TPU v7x, 32 devices: a whole 2x2x4 slice. The times are simulated.
32 devices in a mesh: grp: 4 (over y, x), tp: 8 (over z, core).
Axes of the slice: x: 2, y: 2, z: 4, core: 2. Of those that a mesh axis runs over, the one named last changes fastest.
Arguments:
- key_cache: bfloat16 [4, 8, 768, 512], P('grp', 'tp'), may hold values from -6 to 6
- value_cache: bfloat16 [4, 8, 768, 512], P('grp', 'tp'), may hold values from -12 to 12
- lengths: int32 [4, 8], P('grp', 'tp'), may hold values from 256 to 768, as said below
- queries: bfloat16 [4, 1, 8, 8192], P('grp', None, 'tp'), may hold values from -12 to 12
- new_keys: bfloat16 [4, 1, 8, 512], P('grp', None, 'tp'), may hold values from -18 to 18
- new_values: bfloat16 [4, 1, 8, 512], P('grp', None, 'tp'), may hold values from -12 to 12
- residual: bfloat16 [4, 1, 8, 8192], P('grp', None, 'tp'), may hold values from -4 to 4
- norm_gain: float32 [8192], replicated, may hold values from 0.25 to 1.75
- gate_weight: bfloat16 [4, 13312, 8192], P('grp', 'tp'), may hold values from -0.0625 to 0.0625
- up_weight: bfloat16 [4, 13312, 8192], P('grp', 'tp'), may hold values from -0.0625 to 0.0625
- down_weight: bfloat16 [4, 13312, 8192], P('grp', 'tp'), may hold values from -0.0390625 to 0.0390625
Outputs:
- mixed: bfloat16 [4, 1, 8, 8192], P('grp', None, 'tp')
Inputs may be any that keep to these rules, and one draw needn't show every extreme that they name: `lengths`: some row has exactly 768 valid positions.
All inputs are finite; a program needn't handle non-finite values.
Results may differ from a plain program's by a relative error of at most 0.005.
Values may be sent and summed in bfloat16 or wider, within the bound.
A program may use at most 128 MiB of HBM per device.

v0:
```python
import jax
import jax.numpy as jnp
from jax import lax
from jax.sharding import PartitionSpec as P

HEADS = 64
HD = 128
KVH = 4
masked_score = -1e30


def feed_rows(normed_rows, gate_weight, up_weight, down_weight):
    numbers = (((1,), (1,)), ((), ()))
    gate_part = lax.dot_general(
        normed_rows, gate_weight[0], numbers, preferred_element_type=jnp.float32
    )
    up_part = lax.dot_general(
        normed_rows, up_weight[0], numbers, preferred_element_type=jnp.float32
    )
    product = (jax.nn.silu(gate_part) * up_part).astype(jnp.bfloat16)
    return jnp.dot(product, down_weight[0], preferred_element_type=jnp.float32)


def local(
    key_cache,
    value_cache,
    lengths,
    queries,
    new_keys,
    new_values,
    residual,
    norm_gain,
    gate_weight,
    up_weight,
    down_weight,
):
    groups = lax.axis_size("grp")
    members = lax.axis_size("tp")
    serving = lax.axis_index("grp") < groups // 2
    step_count = queries.shape[1]
    own_rows = queries.shape[2]
    model_width = queries.shape[3]
    head_share = HEADS // KVH
    slot_count = key_cache.shape[2]
    score_scale = HD ** (-0.5)
    own_heads = queries[0].reshape(step_count, own_rows, KVH, head_share, HD)
    cache_keys = key_cache[0].reshape(own_rows, slot_count, KVH, HD)
    cache_values = value_cache[0].reshape(own_rows, slot_count, KVH, HD)
    positions = jnp.arange(slot_count)
    usable = positions[None, :] < lengths[0][:, None]
    usable_mask = usable[None, :, None, None, :]
    cache_scores = (
        jnp.einsum("srjgd,rpjd->srjgp", own_heads, cache_keys, preferred_element_type=jnp.float32)
        * score_scale
    )
    cache_scores = jnp.where(usable_mask, cache_scores, masked_score)
    fresh_keys = new_keys[0].reshape(step_count, own_rows, KVH, HD)
    fresh_values = new_values[0].reshape(step_count, own_rows, KVH, HD)
    fresh_scores = (
        jnp.einsum("srjgd,trjd->srjgt", own_heads, fresh_keys, preferred_element_type=jnp.float32)
        * score_scale
    )
    causal = jnp.arange(step_count)[:, None] >= jnp.arange(step_count)[None, :]
    causal_mask = causal[:, None, None, None, :]
    fresh_scores = jnp.where(causal_mask, fresh_scores, masked_score)
    ceiling = jnp.maximum(jnp.max(cache_scores, axis=-1), jnp.max(fresh_scores, axis=-1))
    cache_exp = jnp.where(usable_mask, jnp.exp(cache_scores - ceiling[..., None]), 0.0)
    fresh_exp = jnp.where(causal_mask, jnp.exp(fresh_scores - ceiling[..., None]), 0.0)
    denominator = jnp.sum(cache_exp, axis=-1) + jnp.sum(fresh_exp, axis=-1)
    cache_weighted = jnp.einsum(
        "srjgp,rpjd->srjgd",
        cache_exp.astype(jnp.bfloat16),
        cache_values,
        preferred_element_type=jnp.float32,
    )
    fresh_weighted = jnp.einsum(
        "srjgt,trjd->srjgd",
        fresh_exp.astype(jnp.bfloat16),
        fresh_values,
        preferred_element_type=jnp.float32,
    )
    attended = (cache_weighted + fresh_weighted) / denominator[..., None]
    attended = attended.reshape(step_count, own_rows, model_width)
    hidden = residual[0].astype(jnp.float32) + attended
    spread_sq = jnp.mean(hidden * hidden, axis=-1, keepdims=True)
    normed = (hidden * lax.rsqrt(spread_sq + 1e-05) * norm_gain).astype(jnp.bfloat16)
    block_rows = step_count * own_rows
    flat_rows = normed.reshape(block_rows, model_width)
    ffn_first = groups // 2
    group_block = lax.all_gather(flat_rows, "tp", axis=0, tiled=True).reshape(
        members, block_rows, model_width
    )
    all_rows = lax.all_gather(group_block, "grp", axis=1, tiled=True)
    real_rows = all_rows[:, : ffn_first * block_rows].reshape(
        members * ffn_first * block_rows, model_width
    )
    within = lax.psum_scatter(
        lax.cond(
            serving,
            lambda operand: jnp.zeros(
                (ffn_first * block_rows * lax.axis_size("tp"), model_width), jnp.float32
            ),
            lambda operand: feed_rows(operand, gate_weight, up_weight, down_weight),
            real_rows,
        ),
        "tp",
        scatter_dimension=0,
        tiled=True,
    )
    padded = jnp.concatenate(
        [within, jnp.zeros(((groups - ffn_first) * block_rows, model_width), jnp.float32)], 0
    )
    summed = lax.psum_scatter(padded, "grp", scatter_dimension=0, tiled=True)
    mixed = (hidden + summed.reshape(step_count, own_rows, model_width)).astype(jnp.bfloat16)
    mixed = jnp.where(serving, mixed, jnp.zeros_like(mixed))
    return mixed[None]


def solution(mesh):
    return jax.shard_map(
        local,
        mesh=mesh,
        in_specs=(
            P("grp", "tp", None, None),
            P("grp", "tp", None, None),
            P("grp", "tp"),
            P("grp", None, "tp", None),
            P("grp", None, "tp", None),
            P("grp", None, "tp", None),
            P("grp", None, "tp", None),
            P(),
            P("grp", "tp", None),
            P("grp", "tp", None),
            P("grp", "tp", None),
        ),
        out_specs=P("grp", None, "tp", None),
        check_vma=False,
    )
```

profile of v0, /device:TPU:0, one launch (start us, length us, event | category | flops | bytes accessed | tf_op | source)
XLA Modules:
  0.0 188.5 jit_solution(14599634890557836540)
XLA Ops:
  6.5 0.0 copy-start
  6.5 0.0 all-reduce.6.cloned.1.call-start
  7.2 1.8 reshape.145
  9.0 0.1 reduce.4
  9.1 0.8 fusion.38
  9.9 0.4 fusion.42
  10.3 0.2 fusion.28
  10.5 0.8 convert_element_type.47
  11.3 1.8 reshape.149
  13.1 0.7 convert.12
  13.8 0.9 fusion.37
  15.3 0.8 multiply_convert_fusion
  16.1 15.7 %all-gather = bf16[65536]{0:T(1024)(128)(2,1)S(1)} all-gather(bf16[8192]{0:T(1024)(128)(2,1)S(1)} %multiply_convert_fusion), channel_id=2, replica_groups=mesh['grp'=4,'tp'=8] {'tp'}, dimensions={0}, use_global_device_ids=true | all-gather | bytes 147456 | tf_op jit(solution)/shard_map/all_gather | solution.py:90
  31.8 0.1 reshape.161
  31.9 10.3 %all-gather.1 = bf16[8,32768]{1,0:T(8,128)(2,1)S(1)} all-gather(bf16[8,8192]{1,0:T(8,128)(2,1)S(1)} %reshape.161), channel_id=3, replica_groups=mesh['grp'=4,'tp'=8] {'grp'}, dimensions={1}, use_global_device_ids=true | all-gather | bytes 655360 | tf_op jit(solution)/shard_map/all_gather | solution.py:93
  42.2 0.4 reshape.162
  42.6 0.0 copy-start.5
  42.6 0.0 copy-start.4
  42.6 0.0 copy-start.3
  42.7 0.1 conditional.1
  42.7 0.0 copy-start.1
  42.7 0.8 copy-done.2
  43.5 0.0 all-reduce.6.cloned.1.call-update
  43.6 0.0 all-reduce.8.cloned.1.call-start
  43.6 0.6 dynamic-slice
  44.9 90.4 %all-reduce.6.cloned.1.call-done = f32[16,8192]{1,0:T(8,128)} async-done(((f32[16,8192]{1,0:T(8,128)}), f32[16,8192]{1,0:T(8,128)}) %all-reduce.6.cloned.1.call-update) | async-done | bytes 524304
  135.3 1.0 constant_dynamic-slice_fusion
  136.3 0.7 concatenate.3
  137.0 0.0 all-reduce.8.cloned.1.call-update
  137.0 0.6 dynamic-slice.2
  137.6 41.8 %all-reduce.8.cloned.1.call-done = f32[4,8192]{1,0:T(4,128)} async-done(((f32[4,8192]{1,0:T(4,128)}), f32[4,8192]{1,0:T(4,128)}) %all-reduce.8.cloned.1.call-update) | async-done | bytes 131088
  179.5 2.2 %broadcast_select_fusion = bf16[1,1,1,8192]{3,2,1,0:T(2,128)(2,1)} fusion(pred[]{:T(512)S(6)} %lt.19, f32[4,8192]{1,0:T(4,128)} %all-reduce.8.cloned.1.call-done, u32[]{:T(128)} %bitcast.23, f32[1,1,1,8192]{3,2,1,0:T(1,128)S(1)} %bitcast.74, bf16[1,1,1,8192]{3,2,1,0:T(2,128)(2,1)S(1)} %copy-done.3), kind=kLoop, calls=%fused_computation.31 | loop fusion | flops 40960 | bytes 98309 | tf_op jit(solution)/shard_map/jit(_where)/select_n | solution.py:115
  (10 shorter events, 0.1 us)
Async XLA Ops:
  6.5 2.4 %copy-start = (bf16[1,1,1,8192]{3,2,1,0:T(2,128)(2,1)S(1)}, bf16[1,1,1,8192]{3,2,1,0:T(2,128)(2,1)}, u32[]{:S(2)}) copy-start(bf16[1,1,1,8192]{3,2,1,0:T(2,128)(2,1)} %param.16) | copy-start | bytes 49156
  6.5 128.8 %all-reduce.6.cloned.1.call-start = ((), (), s32[]{:S(2)}) async-start(), calls=%async_computation | async-start | bytes 1048576
  42.6 1.0 copy-start.5
  42.6 94.4 %copy-start.4 = (u32[32]{0:T(128)S(1)}, u32[32]{0:T(128)}, u32[]{:S(2)}) copy-start(u32[32]{0:T(128)} %constant.51) | copy-start | bytes 388
  42.6 136.8 %copy-start.3 = (bf16[1,1,1,8192]{3,2,1,0:T(2,128)(2,1)S(1)}, bf16[1,1,1,8192]{3,2,1,0:T(2,128)(2,1)}, u32[]{:S(2)}) copy-start(bf16[1,1,1,8192]{3,2,1,0:T(2,128)(2,1)} %param.19) | copy-start | bytes 49156
  42.7 0.8 copy-start.2
  42.7 139.0 %copy-start.1 = (bf16[1,1,1,8192]{3,2,1,0:T(2,128)(2,1)S(1)}, bf16[1,1,1,8192]{3,2,1,0:T(2,128)(2,1)}, u32[]{:S(2)}) copy-start(bf16[1,1,1,8192]{3,2,1,0:T(2,128)(2,1)} %param.16) | copy-start | bytes 49156
  43.6 135.9 %all-reduce.8.cloned.1.call-start = ((), (), s32[]{:S(2)}) async-start(), calls=%async_computation.1 | async-start | bytes 262144
Sparse Core Ops, SparseCore 0:
  43.7 91.5 all-reduce.5
  138.2 41.2 all-reduce.7
where the time goes:
time: 189 us
  waiting for transfers between devices  132 us (70%)
  blocking collectives  26 us (14%)
  between operations  15.5 us (8%)
  local copies, waits for them, and re-layouts  7.69 us (4%)
  other arithmetic  4.78 us (3%)
  matrix products  2.09 us (1%)
    unnamed x4, waiting for transfers between devices  132 us
    all_gather x1, blocking collectives, local(): lax.all_gather(flat_rows, 'tp', axis=0, tiled=True)  15.7 us
    all_gather x1, blocking collectives, local(): all_rows = lax.all_gather(group_block, 'grp', axis=1, tiled=True)  10.3 us
  transfers between devices with their start and end apart: 2, of which 2 were waited for; matrix products, arithmetic and copies ran while one was open for 1% of the time, Pallas kernels for 0%

commit v1 on v0

--- a/solution.py
+++ b/solution.py
@@ -7,6 +7,12 @@
 HD = 128
 KVH = 4
 masked_score = -1e30
+
+
+def gather_by_exchange(x, axis, dim):
+    count = lax.axis_size(axis)
+    repeats = [count if d == dim else 1 for d in range(x.ndim)]
+    return lax.all_to_all(jnp.tile(x, repeats), axis, split_axis=dim, concat_axis=dim, tiled=True)
 
 
 def feed_rows(normed_rows, gate_weight, up_weight, down_weight):
@@ -87,9 +93,7 @@
     block_rows = step_count * own_rows
     flat_rows = normed.reshape(block_rows, model_width)
     ffn_first = groups // 2
-    group_block = lax.all_gather(flat_rows, "tp", axis=0, tiled=True).reshape(
-        members, block_rows, model_width
-    )
+    group_block = gather_by_exchange(flat_rows, "tp", 0).reshape(members, block_rows, model_width)
     all_rows = lax.all_gather(group_block, "grp", axis=1, tiled=True)
     real_rows = all_rows[:, : ffn_first * block_rows].reshape(
         members * ffn_first * block_rows, model_width

time: 189 us -> 187 us (0.989)
  blocking collectives: 26 us -> 10 us
  starting transfers between devices: 0.04 us -> 6.43 us
  waiting for transfers between devices: 132 us -> 138 us
    all_gather x1 -> x0, blocking collectives: 15.7 us -> none  [local(): lax.all_gather(flat_rows, 'tp', axis=0, tiled=True)]
    all_to_all x0 -> x1, waiting for transfers between devices: none -> 6.7 us  [gather_by_exchange(): lax.all_to_all(jnp.tile(x, repeats), axis, split_axis=dim, concat_axis=di...]
    all_to_all x0 -> x1, starting transfers between devices: none -> 6.35 us  [gather_by_exchange(): lax.all_to_all(jnp.tile(x, repeats), axis, split_axis=dim, concat_axis=di...]
    unnamed x15 -> x17, local copies, waits for them, and re-layouts: 3.03 us -> 3.86 us
    another operation x3 -> x5, local copies, waits for them, and re-layouts: 3.54 us -> 4.19 us
  transfers between devices with their start and end apart: 2 -> 3, of which waited for: 2 -> 3; matrix products, arithmetic and copies ran while one was open for 1% -> 1% of each run, Pallas kernels for 0% -> 0%
where the time goes in v1:
time: 187 us
  waiting for transfers between devices  138 us (74%)
  between operations  15.6 us (8%)
  blocking collectives  10 us (5%)
  local copies, waits for them, and re-layouts  8.87 us (5%)
  starting transfers between devices  6.43 us (3%)
  other arithmetic  6.19 us (3%)
  matrix products  2.09 us (1%)
    unnamed x4, waiting for transfers between devices  131 us
    all_gather x1, blocking collectives, local(): all_rows = lax.all_gather(group_block, 'grp', axis=1, tiled=True)  10 us
    all_to_all x1, waiting for transfers between devices, gather_by_exchange(): lax.all_to_all(jnp.tile(x, repeats), axis, split_axis=dim, concat_axis=di...  6.7 us
    all_to_all x1, starting transfers between devices, gather_by_exchange(): lax.all_to_all(jnp.tile(x, repeats), axis, split_axis=dim, concat_axis=di...  6.35 us
    unnamed x17, local copies, waits for them, and re-layouts  3.86 us
  transfers between devices with their start and end apart: 3, of which 3 were waited for; matrix products, arithmetic and copies ran while one was open for 1% of the time, Pallas kernels for 0%

profile of v1, /device:TPU:0, one launch (start us, length us, event | category | flops | bytes accessed | tf_op | source)
XLA Modules:
  0.0 186.9 jit_solution(13162828479628622460)
XLA Ops:
  7.2 1.8 reshape.149
  9.0 0.1 reduce.4
  9.1 0.8 fusion.38
  9.9 0.4 fusion.42
  10.3 0.2 fusion.28
  10.5 0.8 convert_element_type.47
  11.3 1.8 reshape.153
  13.1 0.7 convert.12
  13.7 0.9 fusion.37
  15.3 0.8 multiply_convert_fusion
  16.1 0.1 tile.2
  16.2 0.5 broadcast.50
  16.8 1.4 reduce.5
  18.2 0.7 reshape.169
  18.9 6.4 %all-to-all-start = ((bf16[8,2,4096]{2,1,0:T(2,128)(2,1)}), bf16[8,2,4096]{2,1,0:T(2,128)(2,1)S(1)}, u32[]{:S(2)}, u32[]{:S(2)}) async-start(bf16[8,2,4096]{2,1,0:T(2,128)(2,1)} %reshape.169), calls=%async_computation | async-start | bytes 262144 | tf_op jit(solution)/shard_map/all_to_all | solution.py:15
  25.2 0.0 all-reduce.6.cloned.1.call-start
  25.3 6.7 %all-to-all-done = bf16[8,2,4096]{2,1,0:T(2,128)(2,1)S(1)} async-done(((bf16[8,2,4096]{2,1,0:T(2,128)(2,1)}), bf16[8,2,4096]{2,1,0:T(2,128)(2,1)S(1)}, u32[]{:S(2)}, u32[]{:S(2)}) %all-to-all-start) | async-done | bytes 131104 | tf_op jit(solution)/shard_map/all_to_all | solution.py:15
  32.0 0.1 reshape.170
  32.1 0.2 copy.22
  32.3 10.0 %all_gather.3 = bf16[8,4,8192]{2,0,1:T(8,128)(2,1)S(1)} all-gather(bf16[8,1,8192]{2,0,1:T(8,128)(2,1)S(1)} %copy.22), channel_id=1, replica_groups=mesh['grp'=4,'tp'=8] {'grp'}, dimensions={1}, use_global_device_ids=true | all-gather | bytes 655360 | tf_op jit(solution)/shard_map/all_gather | solution.py:97
  42.3 0.1 conditional.1
  42.4 0.8 copy-done.2
  43.2 0.0 all-reduce.6.cloned.1.call-update
  43.2 0.0 all-reduce.8.cloned.1.call-start
  43.3 0.6 dynamic-slice
  44.5 89.1 %all-reduce.6.cloned.1.call-done = f32[16,8192]{1,0:T(8,128)} async-done(((f32[16,8192]{1,0:T(8,128)}), f32[16,8192]{1,0:T(8,128)}) %all-reduce.6.cloned.1.call-update) | async-done | bytes 524304
  133.7 1.0 constant_dynamic-slice_fusion
  134.6 0.7 concatenate.3
  135.3 0.0 all-reduce.8.cloned.1.call-update
  135.4 0.6 dynamic-slice.2
  136.0 41.8 %all-reduce.8.cloned.1.call-done = f32[4,8192]{1,0:T(4,128)} async-done(((f32[4,8192]{1,0:T(4,128)}), f32[4,8192]{1,0:T(4,128)}) %all-reduce.8.cloned.1.call-update) | async-done | bytes 131088
  177.8 2.2 %broadcast_select_fusion = bf16[1,1,1,8192]{3,2,1,0:T(2,128)(2,1)} fusion(pred[]{:T(512)S(6)} %lt.19, f32[4,8192]{1,0:T(4,128)} %all-reduce.8.cloned.1.call-done, u32[]{:T(128)} %bitcast.23, f32[1,1,1,8192]{3,2,1,0:T(1,128)S(1)} %bitcast.74, bf16[1,1,1,8192]{3,2,1,0:T(2,128)(2,1)S(1)} %copy-done.3), kind=kLoop, calls=%fused_computation.31 | loop fusion | flops 40960 | bytes 98309 | tf_op jit(solution)/shard_map/jit(_where)/select_n | solution.py:119
  (15 shorter events, 0.1 us)
Async XLA Ops:
  6.5 2.4 %copy-start = (bf16[1,1,1,8192]{3,2,1,0:T(2,128)(2,1)S(1)}, bf16[1,1,1,8192]{3,2,1,0:T(2,128)(2,1)}, u32[]{:S(2)}) copy-start(bf16[1,1,1,8192]{3,2,1,0:T(2,128)(2,1)} %param.16) | copy-start | bytes 49156
  18.9 13.1 %all-to-all-start = ((bf16[8,2,4096]{2,1,0:T(2,128)(2,1)}), bf16[8,2,4096]{2,1,0:T(2,128)(2,1)S(1)}, u32[]{:S(2)}, u32[]{:S(2)}) async-start(bf16[8,2,4096]{2,1,0:T(2,128)(2,1)} %reshape.169), calls=%async_computation | async-start | bytes 262144 | tf_op jit(solution)/shard_map/all_to_all | solution.py:15
  25.2 108.4 %all-reduce.6.cloned.1.call-start = ((), (), s32[]{:S(2)}) async-start(), calls=%async_computation.1 | async-start | bytes 1048576
  42.3 1.0 copy-start.5
  42.3 93.0 %copy-start.4 = (u32[32]{0:T(128)S(1)}, u32[32]{0:T(128)}, u32[]{:S(2)}) copy-start(u32[32]{0:T(128)} %constant.51) | copy-start | bytes 388
  42.3 135.5 %copy-start.3 = (bf16[1,1,1,8192]{3,2,1,0:T(2,128)(2,1)S(1)}, bf16[1,1,1,8192]{3,2,1,0:T(2,128)(2,1)}, u32[]{:S(2)}) copy-start(bf16[1,1,1,8192]{3,2,1,0:T(2,128)(2,1)} %param.19) | copy-start | bytes 49156
  42.4 0.8 copy-start.2
  42.4 137.6 %copy-start.1 = (bf16[1,1,1,8192]{3,2,1,0:T(2,128)(2,1)S(1)}, bf16[1,1,1,8192]{3,2,1,0:T(2,128)(2,1)}, u32[]{:S(2)}) copy-start(bf16[1,1,1,8192]{3,2,1,0:T(2,128)(2,1)} %param.16) | copy-start | bytes 49156
  43.2 134.6 %all-reduce.8.cloned.1.call-start = ((), (), s32[]{:S(2)}) async-start(), calls=%async_computation.2 | async-start | bytes 262144
Sparse Core Ops, SparseCore 0:
  43.4 90.2 all-reduce.5
  136.5 41.2 all-reduce.7

commit v2 on v0

--- a/solution.py
+++ b/solution.py
@@ -90,7 +90,18 @@
     group_block = lax.all_gather(flat_rows, "tp", axis=0, tiled=True).reshape(
         members, block_rows, model_width
     )
-    all_rows = lax.all_gather(group_block, "grp", axis=1, tiled=True)
+    devices, index, rows = (lax.axis_size("grp"), lax.axis_index("grp"), group_block.shape[1])
+    ahead = [(i, (i + 1) % devices) for i in range(devices)]
+    out = jnp.zeros(
+        (*group_block.shape[:1], devices * rows, *group_block.shape[1 + 1 :]), group_block.dtype
+    )
+    carried = group_block
+    for turn in range(devices):
+        holder = (index - turn) % devices
+        out = lax.dynamic_update_slice_in_dim(out, carried, holder * rows, axis=1)
+        if turn < devices - 1:
+            carried = lax.ppermute(carried, "grp", ahead)
+    all_rows = out
     real_rows = all_rows[:, : ffn_first * block_rows].reshape(
         members * ffn_first * block_rows, model_width
     )

time: 189 us -> 209 us (1.11)
  waiting for transfers between devices: 132 us -> 160 us
  blocking collectives: 26 us -> 15.7 us
  starting transfers between devices: 0.04 us -> 2.18 us
    ppermute x0 -> x3, waiting for transfers between devices: none -> 16.3 us  [local(): carried = lax.ppermute(carried, 'grp', ahead)]
    unnamed x4, waiting for transfers between devices: 132 us -> 144 us
    all_gather x1 -> x0, blocking collectives: 10.3 us -> none  [local(): all_rows = lax.all_gather(group_block, 'grp', axis=1, tiled=True)]
    ppermute x0 -> x3, starting transfers between devices: none -> 2.14 us  [local(): carried = lax.ppermute(carried, 'grp', ahead)]
  transfers between devices with their start and end apart: 2 -> 5, of which waited for: 2 -> 5; matrix products, arithmetic and copies ran while one was open for 1% -> 1% of each run, Pallas kernels for 0% -> 0%
where the time goes in v2:
time: 209 us; the launch traced here: 208 us
  waiting for transfers between devices  160 us (77%)
  blocking collectives  15.7 us (8%)
  between operations  15.5 us (7%)
  local copies, waits for them, and re-layouts  7.28 us (3%)
  other arithmetic  4.85 us (2%)
  starting transfers between devices  2.18 us (1%)
  matrix products  2.09 us (1%)
    unnamed x4, waiting for transfers between devices  144 us
    ppermute x3, waiting for transfers between devices, local(): carried = lax.ppermute(carried, 'grp', ahead)  16.3 us
    all_gather x1, blocking collectives, local(): lax.all_gather(flat_rows, 'tp', axis=0, tiled=True)  15.7 us
  transfers between devices with their start and end apart: 5, of which 5 were waited for; matrix products, arithmetic and copies ran while one was open for 1% of the time, Pallas kernels for 0%

profile of v2, /device:TPU:0, one launch (start us, length us, event | category | flops | bytes accessed | tf_op | source)
XLA Modules:
  0.0 208.0 jit_solution(15846915504029643104)
XLA Ops:
  7.2 1.8 reshape.145
  9.0 0.1 reduce.4
  9.1 0.8 fusion.38
  9.9 0.4 fusion.42
  10.3 0.2 fusion.28
  10.5 0.8 convert_element_type.47
  11.3 1.8 reshape.149
  13.1 0.7 convert.12
  13.8 0.9 fusion.37
  15.3 0.8 multiply_convert_fusion
  16.1 15.7 %all-gather = bf16[65536]{0:T(1024)(128)(2,1)S(1)} all-gather(bf16[8192]{0:T(1024)(128)(2,1)S(1)} %multiply_convert_fusion), channel_id=2, replica_groups=mesh['grp'=4,'tp'=8] {'tp'}, dimensions={0}, use_global_device_ids=true | all-gather | bytes 147456 | tf_op jit(solution)/shard_map/all_gather | solution.py:90
  31.8 0.1 reshape.154
  31.9 1.5 collective-permute-start
  33.4 5.2 %collective-permute-done = bf16[8,1,8192]{2,0,1:T(8,128)(2,1)S(1)} collective-permute-done((bf16[8,1,8192]{2,0,1:T(8,128)(2,1)S(1)}, bf16[8,1,8192]{2,0,1:T(8,128)(2,1)S(1)}, u32[]{:S(2)}, u32[]{:S(2)}) %collective-permute-start) | collective-permute-done | bytes 131104 | tf_op jit(solution)/shard_map/ppermute | solution.py:103
  38.6 0.6 collective-permute-start.1
  39.2 5.3 %collective-permute-done.1 = bf16[8,1,8192]{2,0,1:T(8,128)(2,1)S(1)} collective-permute-done((bf16[8,1,8192]{2,0,1:T(8,128)(2,1)S(1)}, bf16[8,1,8192]{2,0,1:T(8,128)(2,1)S(1)}, u32[]{:S(2)}, u32[]{:S(2)}) %collective-permute-start.1) | collective-permute-done | bytes 131104 | tf_op jit(solution)/shard_map/ppermute | solution.py:103
  44.5 0.0 collective-permute-start.2
  44.5 5.9 %collective-permute-done.2 = bf16[8,1,8192]{2,0,1:T(8,128)(2,1)S(1)} collective-permute-done((bf16[8,1,8192]{2,0,1:T(8,128)(2,1)S(1)}, bf16[8,1,8192]{2,0,1:T(8,128)(2,1)S(1)}, u32[]{:S(2)}, u32[]{:S(2)}) %collective-permute-start.2) | collective-permute-done | bytes 131104 | tf_op jit(solution)/shard_map/ppermute | solution.py:103
  50.4 0.0 copy-start.1
  50.4 0.8 copy-done.2
  51.2 0.0 all-reduce.6.cloned.1.call-update
  51.2 0.0 all-reduce.8.cloned.1.call-start
  51.3 0.6 dynamic-slice
  52.5 102.2 %all-reduce.6.cloned.1.call-done = f32[16,8192]{1,0:T(8,128)} async-done(((f32[16,8192]{1,0:T(8,128)}), f32[16,8192]{1,0:T(8,128)}) %all-reduce.6.cloned.1.call-update) | async-done | bytes 524304
  154.7 1.0 constant_dynamic-slice_fusion
  155.7 0.7 concatenate.3
  156.4 0.0 all-reduce.8.cloned.1.call-update
  156.4 0.0 copy-done.4
  156.4 0.7 dynamic-slice.2
  157.1 41.8 %all-reduce.8.cloned.1.call-done = f32[4,8192]{1,0:T(4,128)} async-done(((f32[4,8192]{1,0:T(4,128)}), f32[4,8192]{1,0:T(4,128)}) %all-reduce.8.cloned.1.call-update) | async-done | bytes 131088
  198.9 2.3 %broadcast_select_fusion = bf16[1,1,1,8192]{3,2,1,0:T(2,128)(2,1)} fusion(pred[]{:T(512)S(6)} %lt.49, f32[4,8192]{1,0:T(4,128)} %all-reduce.8.cloned.1.call-done, u32[]{:T(128)} %bitcast.23, f32[1,1,1,8192]{3,2,1,0:T(1,128)S(1)} %bitcast.74, bf16[1,1,1,8192]{3,2,1,0:T(2,128)(2,1)S(1)} %copy-done.3), kind=kLoop, calls=%fused_computation.31 | loop fusion | flops 40960 | bytes 98309 | tf_op jit(solution)/shard_map/jit(_where)/select_n | solution.py:126
  201.2 0.0 copy-done.1
  (14 shorter events, 0.1 us)
Async XLA Ops:
  6.5 2.4 %copy-start = (bf16[1,1,1,8192]{3,2,1,0:T(2,128)(2,1)S(1)}, bf16[1,1,1,8192]{3,2,1,0:T(2,128)(2,1)}, u32[]{:S(2)}) copy-start(bf16[1,1,1,8192]{3,2,1,0:T(2,128)(2,1)} %param.16) | copy-start | bytes 49156
  6.5 148.2 %all-reduce.6.cloned.1.call-start = ((), (), s32[]{:S(2)}) async-start(), calls=%async_computation | async-start | bytes 1048576
  31.9 6.7 %collective-permute-start = (bf16[8,1,8192]{2,0,1:T(8,128)(2,1)S(1)}, bf16[8,1,8192]{2,0,1:T(8,128)(2,1)S(1)}, u32[]{:S(2)}, u32[]{:S(2)}) collective-permute-start(bf16[8,1,8192]{2,0,1:T(8,128)(2,1)S(1)} %reshape.154), channel_id=1, source_target_pairs={{0,8},{8,16},{16,24},{24,0},{1,9},{9,17},{17,25},{25,1},{2,10},{10... | collective-permute-start | bytes 393224 | tf_op jit(solution)/shard_map/ppermute | solution.py:103
  38.6 5.9 %collective-permute-start.1 = (bf16[8,1,8192]{2,0,1:T(8,128)(2,1)S(1)}, bf16[8,1,8192]{2,0,1:T(8,128)(2,1)S(1)}, u32[]{:S(2)}, u32[]{:S(2)}) collective-permute-start(bf16[8,1,8192]{2,0,1:T(8,128)(2,1)S(1)} %collective-permute-done), channel_id=1, source_target_pairs={{0,8},{8,16},{16,24},{24,0},{1,9},{9,17},{17,25},{25,1},{2,10},{10... | collective-permute-start | bytes 393224 | tf_op jit(solution)/shard_map/ppermute | solution.py:103
  44.5 5.9 %collective-permute-start.2 = (bf16[8,1,8192]{2,0,1:T(8,128)(2,1)S(1)}, bf16[8,1,8192]{2,0,1:T(8,128)(2,1)S(1)}, u32[]{:S(2)}, u32[]{:S(2)}) collective-permute-start(bf16[8,1,8192]{2,0,1:T(8,128)(2,1)S(1)} %collective-permute-done.1), channel_id=1, source_target_pairs={{0,8},{8,16},{16,24},{24,0},{1,9},{9,17},{17,25},{25,1},{2,10},{10... | collective-permute-start | bytes 393224 | tf_op jit(solution)/shard_map/ppermute | solution.py:103
  50.3 0.9 copy-start.5
  50.3 106.1 %copy-start.4 = (u32[32]{0:T(128)S(1)}, u32[32]{0:T(128)}, u32[]{:S(2)}) copy-start(u32[32]{0:T(128)} %constant.90) | copy-start | bytes 388
  50.3 148.6 %copy-start.3 = (bf16[1,1,1,8192]{3,2,1,0:T(2,128)(2,1)S(1)}, bf16[1,1,1,8192]{3,2,1,0:T(2,128)(2,1)}, u32[]{:S(2)}) copy-start(bf16[1,1,1,8192]{3,2,1,0:T(2,128)(2,1)} %param.19) | copy-start | bytes 49156
  50.4 0.8 copy-start.2
  50.4 150.8 %copy-start.1 = (bf16[1,1,1,8192]{3,2,1,0:T(2,128)(2,1)S(1)}, bf16[1,1,1,8192]{3,2,1,0:T(2,128)(2,1)}, u32[]{:S(2)}) copy-start(bf16[1,1,1,8192]{3,2,1,0:T(2,128)(2,1)} %param.16) | copy-start | bytes 49156
  51.2 147.7 %all-reduce.8.cloned.1.call-start = ((), (), s32[]{:S(2)}) async-start(), calls=%async_computation.1 | async-start | bytes 262144
Sparse Core Ops, SparseCore 0:
  51.3 103.3 all-reduce.5
  157.6 41.2 all-reduce.7
